TPU v7x, 512 devices: a 4x2x32 block of a 4x8x32 slice. The times are simulated.
512 devices in a mesh: group: 2 (over y), seq: 128 (over x, z), head: 2 (over core).
Axes of the slice: x: 4, y: 2, z: 32, core: 2. Of those that a mesh axis runs over, the one named last changes fastest.
The devices are a block of a 4x8x32 slice.
Arguments:
- queries: bfloat16 [32768, 3, 2560], P(('group', 'seq'), None, 'head'), parts along dimension 0, may hold values from -6 to 6, as said below
- keys: bfloat16 [32768, 512], P(('group', 'seq'), 'head'), parts along dimension 0, may hold values from -6 to 6, as said below
- values: bfloat16 [32768, 512], P(('group', 'seq'), 'head'), parts along dimension 0, may hold values from -6 to 6
- lengths: int32 [128], P('group'), parts along dimension 0, may hold values from 1 to 1024, 16384 in all
- page_owner: int32 [8192, 4], P(('group', 'seq'), 'head'), parts along dimension 0, may hold values from 0 to 127, as said below
- page_slot: int32 [8192, 4], P(('group', 'seq'), 'head'), parts along dimension 0, may hold values from 0 to 63, as said below
Outputs:
- attended: bfloat16 [32768, 3, 2560], P(('group', 'seq'), None, 'head'), parts along dimension 0
- cache_pages: bfloat16 [32768, 4, 256], P(('group', 'seq', 'head')), parts along dimension 0
There are 2 independent parts, one for each index of `group`. A program takes and returns all parts, laid end to end along the dimension named above; each array names one. Nothing has to cross between parts.
Inputs may be any that keep to these rules, and one draw needn't show every extreme that they name: `page_owner`: for each index g of the head axis, the pages of KV heads g * 2 to g * 2 + 1 held by one index of seq include at most one page for any one owner, and that bound is reached; every owner receives exactly 64 such pages. `page_slot`: the pages that one owner receives for one index of the head axis have distinct slots. `queries`: entries lie within the range; they are of order one. `keys`: entries lie within the range; they are of order one. `lengths`: sum to 16384; the largest is exactly 1024.
All inputs are finite; a program needn't handle non-finite values.
Results may differ from a plain program's by a relative error of at most 0.0029.
Values may be sent and summed in bfloat16 or wider, within the bound.
No kernel may reach another device: no remote copies, remote signals or barrier semaphores. Data moves between devices by JAX's collectives and lax.ppermute only.
A program may use at most 64 MiB of HBM per device.

v0:
```python
import math

import jax
import jax.numpy as jnp
from jax import lax
from jax.experimental import pallas as pl
from jax.experimental.pallas import tpu as pltpu
from jax.sharding import PartitionSpec as P


QPER = 5
HD = 128
PAGE = 4
CHUNKS = PAGE + 1
NEG = -1e30
PAIR = 2
F32 = jnp.float32
BF16 = jnp.bfloat16

NT = (((1,), (1,)), ((), ()))
NN = (((1,), (0,)), ((), ()))
TN = (((0,), (0,)), ((), ()))


def dot(a, b, dims=NN):
    return lax.dot_general(a, b, dims, preferred_element_type=F32)


def shifted(x, by):
    count = lax.axis_size("seq")
    pairs = [(i, i + by) for i in range(count - by)]
    return lax.ppermute(x, "seq", pairs)


def near_core(x):
    return pltpu.with_memory_space_constraint(x, pltpu.VMEM)


def pack_kernel(keys_ref, vals_ref, owner_ref, slot_ref, own_ref, out_ref):
    for c in range(2):
        own_ref[c * HD : (c + 1) * HD] = keys_ref[:, c * HD : (c + 1) * HD]
        own_ref[(2 + c) * HD : (3 + c) * HD] = vals_ref[:, c * HD : (c + 1) * HD].T
    rows = keys_ref.shape[0]
    pages = rows // PAGE
    per = CHUNKS * 2
    total = out_ref.shape[0]
    page_i = lax.broadcasted_iota(jnp.int32, (pages, rows), 0)
    tok_i = lax.broadcasted_iota(jnp.int32, (pages, rows), 1)
    spread = (tok_i // PAGE == page_i).astype(BF16)
    owner = dot(owner_ref[...].astype(BF16), spread).astype(jnp.int32)
    slot = dot(slot_ref[...].astype(BF16), spread).astype(jnp.int32)
    within = lax.broadcasted_iota(jnp.int32, (1, rows), 1) % PAGE
    keyed, tagged, onehot = [], [], []
    lane_id = lax.broadcasted_iota(jnp.int32, (HD, rows), 0)
    for c in range(2):
        base = owner[c : c + 1] * per
        keyed += [base + within * 2, base + within * 2 + 1]
        tagged.append(jnp.where(within == 0, base + PAGE * 2, -1))
        onehot.append((slot[c : c + 1] == lane_id).astype(BF16))
    parts = []
    for c in range(2):
        parts += [keys_ref[:, c * HD : (c + 1) * HD], vals_ref[:, c * HD : (c + 1) * HD]]
    step = 2 * HD
    for begin in range(0, total, step):
        row = begin + lax.broadcasted_iota(jnp.int32, (step, rows), 0)
        acc = jnp.zeros((step, HD), F32)
        for key, part in zip(keyed, parts):
            acc += dot((row == key).astype(BF16), part)
        for key, hot in zip(tagged, onehot):
            acc += dot((row == key).astype(BF16), hot, NT)
        out_ref[begin : begin + step] = acc.astype(BF16)


def pack_pages(keys, values, owner, slot, seq_count):
    return pl.pallas_call(
        pack_kernel,
        out_shape=(
            pltpu.VMEM((4 * HD, keys.shape[0]), BF16),
            pltpu.VMEM((seq_count * CHUNKS * 2, HD), BF16),
        ),
        name="pack_pages",
    )(keys, values, owner, slot)


def place_kernel(got_ref, out_ref):
    total = got_ref.shape[0]
    per = CHUNKS * 2
    sources = total // per
    pages = PAGE * 2
    slots = out_ref.shape[0] // pages
    got = got_ref[...]
    row = lax.broadcasted_iota(jnp.int32, (1, total), 1)
    source, inside = row // per, row % per
    src = lax.broadcasted_iota(jnp.int32, (sources, 1), 0)
    hot = dot((row == src * per + pages).astype(BF16), got).astype(BF16)[:, :slots]
    chosen = dot(hot, (source == src).astype(BF16), TN).astype(BF16)
    dst = lax.broadcasted_iota(jnp.int32, (slots * pages, 1), 0)
    slot = lax.broadcasted_iota(jnp.int32, (1, slots), 1)
    wide = dot((dst // pages == slot).astype(BF16), chosen).astype(BF16)
    want = (dst % PAGE) * 2 + dst % pages // PAGE
    step = 2 * HD
    for begin in range(0, slots * pages, step):
        here = slice(begin, begin + step)
        placed = jnp.where(want[here] == inside, wide[here], jnp.zeros((), BF16))
        out_ref[here] = dot(placed, got).astype(BF16)


def place_pages(got, slots):
    return pl.pallas_call(
        place_kernel,
        out_shape=jax.ShapeDtypeStruct((slots * PAGE * 2, HD), BF16),
        name="place_pages",
    )(near_core(got))


def attend_kernel(groups, first, final, *refs):
    refs = list(refs)
    mine_ref, lens_ref, q_ref = refs[:3]
    arrays = 1 + max(g[0] for g in groups)
    kv = refs[3 : 3 + arrays]
    rest = refs[3 + arrays :]
    state_in = None if first else rest.pop(0)
    result_ref = rest.pop(0)
    work, sems = rest[:2]
    staged = rest[2] if final else None
    layers, rows, width = q_ref.shape
    wide = QPER * HD
    units = layers * width // wide
    reqs = lens_ref.shape[1]

    def fetch(i):
        return pltpu.make_async_copy(state_in.at[i], work.at[i], sems.at[0, i])

    def send(i):
        if not final:
            return pltpu.make_async_copy(work.at[i], result_ref.at[i], sems.at[1, i])
        lanes = pl.ds(pl.multiple_of(i % (width // wide) * wide, HD), wide)
        return pltpu.make_async_copy(
            staged.at[i], result_ref.at[i // (width // wide), :, lanes], sems.at[1, i]
        )

    if not first:
        for i in range(units):
            fetch(i).start()

    base = mine_ref[0] * rows
    lens = jnp.broadcast_to(lens_ref[...], (reqs, reqs)).astype(F32)
    r_i = lax.broadcasted_iota(jnp.int32, (reqs, reqs), 0)
    e_i = lax.broadcasted_iota(jnp.int32, (reqs, reqs), 1)
    starts = jnp.sum(jnp.where(e_i < r_i, lens, 0.0), axis=1, keepdims=True) - base.astype(F32)
    lane = lax.broadcasted_iota(jnp.int32, (1, rows), 1)
    known = jnp.where(starts <= lane.astype(F32), starts, -3e7)
    begin = jnp.max(known, axis=0, keepdims=True).astype(jnp.int32)
    earliest = jnp.min(begin)
    factor = math.log2(math.e) / math.sqrt(HD)

    def take(some, i):
        head = i % (width // wide)
        layer = i // (width // wide)
        if not first:
            old = work[i, HD : HD + 1]
            old_total = work[i, HD + 8 : HD + 9]
        if some:
            key_i = lax.broadcasted_iota(jnp.int32, (rows, rows), 0)
            qry_i = lax.broadcasted_iota(jnp.int32, (rows, rows), 1)
            keys, vals, masks = [], [], []
            for source, index, distance in some:
                at = pl.multiple_of((4 * index + head) * HD, HD)
                keys.append(kv[source][pl.ds(at, HD)])
                vals.append(kv[source][pl.ds(at + 2 * HD, HD)])
                inside = key_i >= begin + distance * rows
                masks.append(inside & (key_i <= qry_i) if distance == 0 else inside)
            v_all = jnp.concatenate(vals, axis=1)
            lanes = [pl.ds(pl.multiple_of((head * QPER + q) * HD, HD), HD) for q in range(QPER)]
            queries = jnp.concatenate([q_ref[layer, :, at] for at in lanes], axis=0)
            scores = dot(jnp.concatenate(keys, axis=0), queries, NT) * factor
            allowed = jnp.concatenate([jnp.concatenate(masks, axis=0)] * QPER, axis=1)
            scores = jnp.where(allowed, scores, NEG)
            top = jnp.max(scores, axis=0, keepdims=True)
            if not first:
                top = jnp.maximum(old, top)
            weights = jnp.exp2(scores - top)
            total = jnp.sum(weights, axis=0, keepdims=True)
            acc = dot(v_all, weights.astype(BF16))
            if not first:
                shrink = jnp.exp2(old - top)
                total += old_total * shrink
                acc += work[i, :HD] * shrink
        if final:
            if not some:
                total, acc = old_total, work[i, :HD]
            normed = (acc * (1.0 / total)).astype(BF16)
            for q in range(QPER):
                staged[i, :, q * HD : (q + 1) * HD] = normed[:, q * rows : (q + 1) * rows].T
        elif some:
            work[i, :HD] = acc
            work[i, HD : HD + 8] = jnp.broadcast_to(top, (8, wide))
            work[i, HD + 8 :] = jnp.broadcast_to(total, (8, wide))

    for used in range(1 if first else 0, len(groups) + 1):
        some = groups[:used]
        case = True
        if used and some[-1][2]:
            case = earliest < rows - some[-1][2] * rows
        if used < len(groups):
            case = jnp.logical_and(case, earliest >= rows - groups[used][2] * rows)

        @pl.when(case)
        def _(some=some):
            @pl.loop(0, units, step=PAIR)
            def _(i):
                for j in range(PAIR):
                    if not first:
                        fetch(i + j).wait()
                for j in range(PAIR):
                    take(some, i + j)
                for j in range(PAIR):
                    send(i + j).start()

    for i in range(units):
        send(i).wait()


def attend(mine, lengths, queries, arrays, groups, state, final):
    layers, rows, width = queries.shape
    units = layers * width // (QPER * HD)
    first = state is None
    in_specs = [
        pl.BlockSpec(memory_space=pltpu.SMEM),
        pl.BlockSpec(memory_space=pltpu.VMEM),
        pl.BlockSpec(memory_space=pltpu.VMEM),
    ]
    in_specs += [pl.BlockSpec(memory_space=pltpu.VMEM) for _ in arrays]
    kept = (units, HD + 16, QPER * rows)
    operands = [mine, lengths, near_core(queries), *map(near_core, arrays)]
    if not first:
        in_specs.append(pl.BlockSpec(memory_space=pl.ANY))
        operands.append(state)
    scratch = [pltpu.VMEM(kept, F32), pltpu.SemaphoreType.DMA((2, units))]
    if final:
        scratch.append(pltpu.VMEM((units, rows, QPER * HD), BF16))
        out_shape = jax.ShapeDtypeStruct(queries.shape, BF16)
    else:
        out_shape = jax.ShapeDtypeStruct(kept, F32)

    def kernel(*refs):
        attend_kernel(groups, first, final, *refs)

    return pl.pallas_call(
        kernel,
        in_specs=in_specs,
        out_specs=pl.BlockSpec(memory_space=pl.ANY),
        out_shape=out_shape,
        scratch_shapes=scratch,
        name="attend_last" if final else "attend_part",
    )(*operands)


def shards(queries, keys, values, lengths, page_owner, page_slot):
    tok_rows = keys.shape[0]
    slots = tok_rows // PAGE * 2
    seq_count = lax.axis_size("seq")
    mine = lax.axis_index("seq").astype(jnp.int32).reshape(1)
    lens = lengths.reshape(1, -1)
    flat_q = queries.transpose(1, 0, 2)

    own, outgoing = pack_pages(keys, values, page_owner.T, page_slot.T, seq_count)
    b6 = shifted(own, 6)
    b3 = shifted(own, 3)
    b1 = shifted(own, 1)

    got = lax.all_to_all(
        outgoing.reshape(seq_count, CHUNKS, 2, HD), "seq", split_axis=0, concat_axis=0, tiled=True
    )

    b47 = shifted(jnp.concatenate([b3, b6]), 1)
    b2 = shifted(b1, 1)
    groups = [(0, 0, 0), (1, 0, 1), (2, 0, 3), (3, 0, 6)]
    state = attend(mine, lens, flat_q, [own, b1, b3, b6], groups, None, False)
    b58 = shifted(b47, 1)
    groups = [(0, 0, 2), (1, 0, 4), (1, 1, 7)]
    state = attend(mine, lens, flat_q, [b2, b47], groups, state, False)
    out = attend(mine, lens, flat_q, [b58], [(0, 0, 5), (0, 1, 8)], state, True)
    attended = out.transpose(1, 0, 2)

    placed = place_pages(got.reshape(seq_count * CHUNKS * 2, HD), slots)
    cache_pages = (
        placed.reshape(slots, 2, PAGE, HD).transpose(0, 2, 1, 3).reshape(slots, PAGE, 2 * HD)
    )
    return (attended, cache_pages)


def solution(mesh):
    placed = (
        P(("group", "seq"), None, "head"),
        P(("group", "seq"), "head"),
        P(("group", "seq"), "head"),
        P("group"),
        P(("group", "seq"), "head"),
        P(("group", "seq"), "head"),
    )
    return jax.shard_map(
        shards,
        mesh=mesh,
        in_specs=placed,
        out_specs=(P(("group", "seq"), None, "head"), P(("group", "seq", "head"), None, None)),
        check_vma=False,
    )
```

profile of v0, /device:TPU:46, one launch (start us, length us, event | category | flops | bytes accessed | tf_op | source)
XLA Modules:
  0.0 147.4 jit_solution(447506649915047427)
XLA Ops:
  0.6 2.4 %pack_pages.1 = (bf16[512,128]{1,0:T(8,128)(2,1)S(1)}, bf16[1280,128]{1,0:T(8,128)(2,1)}) custom-call(bf16[128,256]{1,0:T(8,128)(2,1)} %keys_ref.1, bf16[128,256]{1,0:T(8,128)(2,1)} %vals_ref.1, s32[2,32]{1,0:T(2,128)} %bitcast.22, s32[2,32]{1,0:T(2,128)} %bitcast.23), custom_call_target="tpu_custom_call" | custom-call | tf_op jit(solution)/shard_map/pack_pages/pallas_call | solution.py:75
  3.0 0.0 copy-start.1
  3.0 52.3 %all-to-all-start = ((bf16[128,5,2,128]{3,2,1,0:T(2,128)(2,1)}), bf16[128,5,2,128]{3,2,1,0:T(2,128)(2,1)S(1)}, u32[]{:S(2)}, u32[]{:S(2)}) async-start(bf16[128,5,2,128]{3,2,1,0:T(2,128)(2,1)} %bitcast.6), calls=%async_computation | async-start | bytes 655360 | tf_op jit(solution)/shard_map/all_to_all | solution.py:272
  55.4 5.3 %collective-permute-start = (bf16[512,128]{1,0:T(8,128)(2,1)S(1)}, bf16[512,128]{1,0:T(8,128)(2,1)S(1)}, u32[]{:S(2)}, u32[]{:S(2)}) collective-permute-start(bf16[512,128]{1,0:T(8,128)(2,1)S(1)} %get-tuple-element.4.refs_3_), channel_id=1, source_target_pairs={{0,6},{2,8},{4,10},{6,12},{8,14},{10,16},{12,18},{14,20},{16,22},{... | collective-permute-start | bytes 393224 | tf_op jit(solution)/shard_map/ppermute | solution.py:32
  60.6 10.4 %collective-permute-start.1 = (bf16[512,128]{1,0:T(8,128)(2,1)S(1)}, bf16[512,128]{1,0:T(8,128)(2,1)S(1)}, u32[]{:S(2)}, u32[]{:S(2)}) collective-permute-start(bf16[512,128]{1,0:T(8,128)(2,1)S(1)} %get-tuple-element.4.refs_3_), channel_id=1, source_target_pairs={{0,12},{2,14},{4,16},{6,18},{8,20},{10,22},{12,24},{14,26},{16,28}... | collective-permute-start | bytes 393224 | tf_op jit(solution)/shard_map/ppermute | solution.py:32
  71.1 25.2 %collective-permute-done.refs_5_ = bf16[512,128]{1,0:T(8,128)(2,1)S(1)} collective-permute-done((bf16[512,128]{1,0:T(8,128)(2,1)S(1)}, bf16[512,128]{1,0:T(8,128)(2,1)S(1)}, u32[]{:S(2)}, u32[]{:S(2)}) %collective-permute-start) | collective-permute-done | bytes 131104 | tf_op jit(solution)/shard_map/ppermute | solution.py:32
  96.3 14.0 %collective-permute-done.1.refs_6_ = bf16[512,128]{1,0:T(8,128)(2,1)S(1)} collective-permute-done((bf16[512,128]{1,0:T(8,128)(2,1)S(1)}, bf16[512,128]{1,0:T(8,128)(2,1)S(1)}, u32[]{:S(2)}, u32[]{:S(2)}) %collective-permute-start.1) | collective-permute-done | bytes 131104 | tf_op jit(solution)/shard_map/ppermute | solution.py:32
  110.2 4.3 %collective-permute-start.2 = (bf16[1024,128]{1,0:T(8,128)(2,1)S(1)}, bf16[1024,128]{1,0:T(8,128)(2,1)S(1)}, u32[]{:S(2)}, u32[]{:S(2)}) collective-permute-start(bf16[1024,128]{1,0:T(8,128)(2,1)S(1)} %pad_maximum_fusion), channel_id=1, source_target_pairs={{0,2},{2,4},{4,6},{6,8},{8,10},{10,12},{12,14},{14,16},{16,18},{18... | collective-permute-start | bytes 786440 | tf_op jit(solution)/shard_map/ppermute | solution.py:32
  114.6 2.6 %collective-permute-start.4 = (bf16[512,128]{1,0:T(8,128)(2,1)S(1)}, bf16[512,128]{1,0:T(8,128)(2,1)S(1)}, u32[]{:S(2)}, u32[]{:S(2)}) collective-permute-start(bf16[512,128]{1,0:T(8,128)(2,1)S(1)} %get-tuple-element.4.refs_3_), channel_id=1, source_target_pairs={{0,2},{2,4},{4,6},{6,8},{8,10},{10,12},{12,14},{14,16},{16,18},{18... | collective-permute-start | bytes 393224 | tf_op jit(solution)/shard_map/ppermute | solution.py:32
  117.2 3.9 %collective-permute-done.2.refs_4_ = bf16[1024,128]{1,0:T(8,128)(2,1)S(1)} collective-permute-done((bf16[1024,128]{1,0:T(8,128)(2,1)S(1)}, bf16[1024,128]{1,0:T(8,128)(2,1)S(1)}, u32[]{:S(2)}, u32[]{:S(2)}) %collective-permute-start.2) | collective-permute-done | bytes 262176 | tf_op jit(solution)/shard_map/ppermute | solution.py:32
  121.1 4.2 %collective-permute-start.3 = (bf16[1024,128]{1,0:T(8,128)(2,1)S(1)}, bf16[1024,128]{1,0:T(8,128)(2,1)S(1)}, u32[]{:S(2)}, u32[]{:S(2)}) collective-permute-start(bf16[1024,128]{1,0:T(8,128)(2,1)S(1)} %collective-permute-done.2.refs_4_), channel_id=1, source_target_pairs={{0,2},{2,4},{4,6},{6,8},{8,10},{10,12},{12,14},{14,16},{16,18},{18... | collective-permute-start | bytes 786440 | tf_op jit(solution)/shard_map/ppermute | solution.py:32
  125.3 0.0 collective-permute-done.4.refs_4_
  125.3 2.2 %collective-permute-start.5 = (bf16[512,128]{1,0:T(8,128)(2,1)S(1)}, bf16[512,128]{1,0:T(8,128)(2,1)S(1)}, u32[]{:S(2)}, u32[]{:S(2)}) collective-permute-start(bf16[512,128]{1,0:T(8,128)(2,1)S(1)} %collective-permute-done.4.refs_4_), channel_id=1, source_target_pairs={{0,2},{2,4},{4,6},{6,8},{8,10},{10,12},{12,14},{14,16},{16,18},{18... | collective-permute-start | bytes 393224 | tf_op jit(solution)/shard_map/ppermute | solution.py:32
  127.6 0.0 copy-start
  127.6 1.2 copy-done
  128.8 5.8 %attend_part.2.refs_5_ = f32[6,144,640]{2,1,0:T(8,128)} custom-call(s32[1]{0:T(128)} %bitcast.refs_0_, s32[1,64]{1,0:T(1,128)} %bitcast.19, bf16[3,128,1280]{2,1,0:T(8,128)(2,1)S(1)} %bitcast.13, bf16[512,128]{1,0:T(8,128)(2,1)S(1)} %get-tuple-element.4.refs_3_, bf16[512,128]{1,0:T(8,128)(2,1)S(1)} %collective-permute-done.4.refs_4_, ...), custom_call_target="tpu_custom_call" | custom-call | tf_op jit(solution)/shard_map/attend_part/pallas_call | solution.py:249
  134.6 0.0 collective-permute-done.5.refs_3_
  134.6 0.0 copy-done.1
  134.6 5.7 %attend_part.3.refs_4_ = f32[6,144,640]{2,1,0:T(8,128)} custom-call(s32[1]{0:T(128)} %bitcast.refs_0_, s32[1,64]{1,0:T(1,128)} %bitcast.20, bf16[3,128,1280]{2,1,0:T(8,128)(2,1)S(1)} %bitcast.14, bf16[512,128]{1,0:T(8,128)(2,1)S(1)} %collective-permute-done.5.refs_3_, bf16[1024,128]{1,0:T(8,128)(2,1)S(1)} %collective-permute-done.2.refs_4_, ...), custom_call_target="tpu_custom_call" | custom-call | tf_op jit(solution)/shard_map/attend_part/pallas_call | solution.py:249
  140.3 0.0 collective-permute-done.3.refs_3_
  140.3 5.1 %attend_last.1 = bf16[3,128,1280]{2,1,0:T(8,128)(2,1)} custom-call(s32[1]{0:T(128)} %bitcast.refs_0_, s32[1,64]{1,0:T(1,128)} %bitcast.21, bf16[3,128,1280]{2,1,0:T(8,128)(2,1)S(1)} %bitcast.15, bf16[1024,128]{1,0:T(8,128)(2,1)S(1)} %collective-permute-done.3.refs_3_, f32[6,144,640]{2,1,0:T(8,128)} %attend_part.3.refs_4_), custom_call_target="tpu_custom_call" | custom-call | tf_op jit(solution)/shard_map/attend_last/pallas_call | solution.py:249
  145.4 0.0 all-to-all-done
  145.5 2.0 %place_pages.1 = bf16[512,128]{1,0:T(8,128)(2,1)} custom-call(bf16[1280,128]{1,0:T(8,128)(2,1)S(1)} %bitcast.16), custom_call_target="tpu_custom_call" | custom-call | tf_op jit(solution)/shard_map/place_pages/pallas_call | solution.py:109
  (1 shorter events, 0.0 us)
Async XLA Ops:
  3.0 131.6 %copy-start.1 = (bf16[128,3,1280]{2,0,1:T(8,128)(2,1)S(1)}, bf16[128,3,1280]{2,0,1:T(8,128)(2,1)}, u32[]{:S(2)}) copy-start(bf16[128,3,1280]{2,0,1:T(8,128)(2,1)} %param.6) | copy-start | bytes 2949124
  3.0 142.4 %all-to-all-start = ((bf16[128,5,2,128]{3,2,1,0:T(2,128)(2,1)}), bf16[128,5,2,128]{3,2,1,0:T(2,128)(2,1)S(1)}, u32[]{:S(2)}, u32[]{:S(2)}) async-start(bf16[128,5,2,128]{3,2,1,0:T(2,128)(2,1)} %bitcast.6), calls=%async_computation | async-start | bytes 655360 | tf_op jit(solution)/shard_map/all_to_all | solution.py:272
  55.4 40.9 %collective-permute-start = (bf16[512,128]{1,0:T(8,128)(2,1)S(1)}, bf16[512,128]{1,0:T(8,128)(2,1)S(1)}, u32[]{:S(2)}, u32[]{:S(2)}) collective-permute-start(bf16[512,128]{1,0:T(8,128)(2,1)S(1)} %get-tuple-element.4.refs_3_), channel_id=1, source_target_pairs={{0,6},{2,8},{4,10},{6,12},{8,14},{10,16},{12,18},{14,20},{16,22},{... | collective-permute-start | bytes 393224 | tf_op jit(solution)/shard_map/ppermute | solution.py:32
  60.6 49.6 %collective-permute-start.1 = (bf16[512,128]{1,0:T(8,128)(2,1)S(1)}, bf16[512,128]{1,0:T(8,128)(2,1)S(1)}, u32[]{:S(2)}, u32[]{:S(2)}) collective-permute-start(bf16[512,128]{1,0:T(8,128)(2,1)S(1)} %get-tuple-element.4.refs_3_), channel_id=1, source_target_pairs={{0,12},{2,14},{4,16},{6,18},{8,20},{10,22},{12,24},{14,26},{16,28}... | collective-permute-start | bytes 393224 | tf_op jit(solution)/shard_map/ppermute | solution.py:32
  110.2 10.9 %collective-permute-start.2 = (bf16[1024,128]{1,0:T(8,128)(2,1)S(1)}, bf16[1024,128]{1,0:T(8,128)(2,1)S(1)}, u32[]{:S(2)}, u32[]{:S(2)}) collective-permute-start(bf16[1024,128]{1,0:T(8,128)(2,1)S(1)} %pad_maximum_fusion), channel_id=1, source_target_pairs={{0,2},{2,4},{4,6},{6,8},{8,10},{10,12},{12,14},{14,16},{16,18},{18... | collective-permute-start | bytes 786440 | tf_op jit(solution)/shard_map/ppermute | solution.py:32
  114.6 10.7 %collective-permute-start.4 = (bf16[512,128]{1,0:T(8,128)(2,1)S(1)}, bf16[512,128]{1,0:T(8,128)(2,1)S(1)}, u32[]{:S(2)}, u32[]{:S(2)}) collective-permute-start(bf16[512,128]{1,0:T(8,128)(2,1)S(1)} %get-tuple-element.4.refs_3_), channel_id=1, source_target_pairs={{0,2},{2,4},{4,6},{6,8},{8,10},{10,12},{12,14},{14,16},{16,18},{18... | collective-permute-start | bytes 393224 | tf_op jit(solution)/shard_map/ppermute | solution.py:32
  121.1 19.2 %collective-permute-start.3 = (bf16[1024,128]{1,0:T(8,128)(2,1)S(1)}, bf16[1024,128]{1,0:T(8,128)(2,1)S(1)}, u32[]{:S(2)}, u32[]{:S(2)}) collective-permute-start(bf16[1024,128]{1,0:T(8,128)(2,1)S(1)} %collective-permute-done.2.refs_4_), channel_id=1, source_target_pairs={{0,2},{2,4},{4,6},{6,8},{8,10},{10,12},{12,14},{14,16},{16,18},{18... | collective-permute-start | bytes 786440 | tf_op jit(solution)/shard_map/ppermute | solution.py:32
  125.3 9.3 %collective-permute-start.5 = (bf16[512,128]{1,0:T(8,128)(2,1)S(1)}, bf16[512,128]{1,0:T(8,128)(2,1)S(1)}, u32[]{:S(2)}, u32[]{:S(2)}) collective-permute-start(bf16[512,128]{1,0:T(8,128)(2,1)S(1)} %collective-permute-done.4.refs_4_), channel_id=1, source_target_pairs={{0,2},{2,4},{4,6},{6,8},{8,10},{10,12},{12,14},{14,16},{16,18},{18... | collective-permute-start | bytes 393224 | tf_op jit(solution)/shard_map/ppermute | solution.py:32
  127.6 1.2 copy-start
where the time goes:
time: 148 us; the launch traced here: 147 us
  starting transfers between devices  81.4 us (55%)
  waiting for transfers between devices  43.1 us (29%)
  Pallas kernels  20.9 us (14%)
    all_to_all x1, starting transfers between devices, shards(): lax.all_to_all(outgoing.reshape(seq_count, CHUNKS, 2, HD), 'seq', split_a...  52.3 us
    ppermute x6, waiting for transfers between devices, shifted(): return lax.ppermute(x, 'seq', pairs)  43.1 us
    ppermute x6, starting transfers between devices, shifted(): return lax.ppermute(x, 'seq', pairs)  29.1 us
    pallas_call x3, Pallas kernels, attend(): pl.pallas_call(kernel, in_specs=in_specs, out_specs=pl.BlockSpec(memory_s...  16.6 us
  transfers between devices with their start and end apart: 7, of which 3 were waited for; matrix products, arithmetic and copies ran while one was open for 0% of the time, Pallas kernels for 11%

commit v1 on v0

--- a/solution.py
+++ b/solution.py
@@ -82,7 +82,7 @@
     )(keys, values, owner, slot)
 
 
-def place_kernel(got_ref, out_ref):
+def place_pages(got_ref, out_ref):
     total = got_ref.shape[0]
     per = CHUNKS * 2
     sources = total // per
@@ -105,14 +105,6 @@
         out_ref[here] = dot(placed, got).astype(BF16)
 
 
-def place_pages(got, slots):
-    return pl.pallas_call(
-        place_kernel,
-        out_shape=jax.ShapeDtypeStruct((slots * PAGE * 2, HD), BF16),
-        name="place_pages",
-    )(near_core(got))
-
-
 def attend_kernel(groups, first, final, *refs):
     refs = list(refs)
     mine_ref, lens_ref, q_ref = refs[:3]
@@ -120,9 +112,10 @@
     kv = refs[3 : 3 + arrays]
     rest = refs[3 + arrays :]
     state_in = None if first else rest.pop(0)
-    result_ref = rest.pop(0)
-    work, sems = rest[:2]
-    staged = rest[2] if final else None
+    if final:
+        got_ref, result_ref, pages_ref, work, sems, staged, placed, page_sem = rest
+    else:
+        result_ref, work, sems = rest
     layers, rows, width = q_ref.shape
     wide = QPER * HD
     units = layers * width // wide
@@ -142,6 +135,10 @@
     if not first:
         for i in range(units):
             fetch(i).start()
+    if final:
+        place_pages(got_ref, placed)
+        pages_out = pltpu.make_async_copy(placed, pages_ref, page_sem)
+        pages_out.start()
 
     base = mine_ref[0] * rows
     lens = jnp.broadcast_to(lens_ref[...], (reqs, reqs)).astype(F32)
@@ -219,12 +216,14 @@
 
     for i in range(units):
         send(i).wait()
-
-
-def attend(mine, lengths, queries, arrays, groups, state, final):
+    if final:
+        pages_out.wait()
+
+
+def attend(mine, lengths, queries, arrays, groups, state, got=None):
     layers, rows, width = queries.shape
     units = layers * width // (QPER * HD)
-    first = state is None
+    first, final = state is None, got is not None
     in_specs = [
         pl.BlockSpec(memory_space=pltpu.SMEM),
         pl.BlockSpec(memory_space=pltpu.VMEM),
@@ -237,11 +236,20 @@
         in_specs.append(pl.BlockSpec(memory_space=pl.ANY))
         operands.append(state)
     scratch = [pltpu.VMEM(kept, F32), pltpu.SemaphoreType.DMA((2, units))]
+    hbm = pl.BlockSpec(memory_space=pl.ANY)
     if final:
-        scratch.append(pltpu.VMEM((units, rows, QPER * HD), BF16))
-        out_shape = jax.ShapeDtypeStruct(queries.shape, BF16)
+        in_specs.append(pl.BlockSpec(memory_space=pltpu.VMEM))
+        operands.append(near_core(got))
+        pages = (rows // PAGE * 2 * PAGE * 2, HD)
+        scratch += [
+            pltpu.VMEM((units, rows, QPER * HD), BF16),
+            pltpu.VMEM(pages, BF16),
+            pltpu.SemaphoreType.DMA,
+        ]
+        out_shape = (jax.ShapeDtypeStruct(queries.shape, BF16), jax.ShapeDtypeStruct(pages, BF16))
+        out_specs = (hbm, hbm)
     else:
-        out_shape = jax.ShapeDtypeStruct(kept, F32)
+        out_shape, out_specs = jax.ShapeDtypeStruct(kept, F32), hbm
 
     def kernel(*refs):
         attend_kernel(groups, first, final, *refs)
@@ -249,7 +257,7 @@
     return pl.pallas_call(
         kernel,
         in_specs=in_specs,
-        out_specs=pl.BlockSpec(memory_space=pl.ANY),
+        out_specs=out_specs,
         out_shape=out_shape,
         scratch_shapes=scratch,
         name="attend_last" if final else "attend_part",
@@ -276,14 +284,13 @@
     b47 = shifted(jnp.concatenate([b3, b6]), 1)
     b2 = shifted(b1, 1)
     groups = [(0, 0, 0), (1, 0, 1), (2, 0, 3), (3, 0, 6)]
-    state = attend(mine, lens, flat_q, [own, b1, b3, b6], groups, None, False)
+    state = attend(mine, lens, flat_q, [own, b1, b3, b6], groups, None)
     b58 = shifted(b47, 1)
     groups = [(0, 0, 2), (1, 0, 4), (1, 1, 7)]
-    state = attend(mine, lens, flat_q, [b2, b47], groups, state, False)
-    out = attend(mine, lens, flat_q, [b58], [(0, 0, 5), (0, 1, 8)], state, True)
+    state = attend(mine, lens, flat_q, [b2, b47], groups, state)
+    got = got.reshape(seq_count * CHUNKS * 2, HD)
+    out, placed = attend(mine, lens, flat_q, [b58], [(0, 0, 5), (0, 1, 8)], state, got)
     attended = out.transpose(1, 0, 2)
-
-    placed = place_pages(got.reshape(seq_count * CHUNKS * 2, HD), slots)
     cache_pages = (
         placed.reshape(slots, 2, PAGE, HD).transpose(0, 2, 1, 3).reshape(slots, PAGE, 2 * HD)
     )

time: 148 us -> 147 us (level)
    pallas_call x4 -> x3, Pallas kernels: 18.6 us -> 17.5 us  [attend(): pl.pallas_call(kernel, in_specs=in_specs, out_specs=out_specs, out_shape=...]
  transfers between devices with their start and end apart: 7 -> 7, of which waited for: 3 -> 3; matrix products, arithmetic and copies ran while one was open for 0% -> 0% of each run, Pallas kernels for 11% -> 8%
where the time goes in v1:
time: 147 us; the launch traced here: 146 us
  starting transfers between devices  81.4 us (55%)
  waiting for transfers between devices  43.1 us (29%)
  Pallas kernels  19.9 us (14%)
    all_to_all x1, starting transfers between devices, shards(): lax.all_to_all(outgoing.reshape(seq_count, CHUNKS, 2, HD), 'seq', split_a...  52.3 us
    ppermute x6, waiting for transfers between devices, shifted(): return lax.ppermute(x, 'seq', pairs)  43.1 us
    ppermute x6, starting transfers between devices, shifted(): return lax.ppermute(x, 'seq', pairs)  29.1 us
    pallas_call x3, Pallas kernels, attend(): pl.pallas_call(kernel, in_specs=in_specs, out_specs=out_specs, out_shape=...  17.5 us
  transfers between devices with their start and end apart: 7, of which 3 were waited for; matrix products, arithmetic and copies ran while one was open for 0% of the time, Pallas kernels for 8%

profile of v1, /device:TPU:46, one launch (start us, length us, event | category | flops | bytes accessed | tf_op | source)
XLA Modules:
  0.0 146.4 jit_solution(7778470093082773604)
XLA Ops:
  0.6 2.4 %pack_pages.1 = (bf16[512,128]{1,0:T(8,128)(2,1)S(1)}, bf16[1280,128]{1,0:T(8,128)(2,1)}) custom-call(bf16[128,256]{1,0:T(8,128)(2,1)} %keys_ref.1, bf16[128,256]{1,0:T(8,128)(2,1)} %vals_ref.1, s32[2,32]{1,0:T(2,128)} %bitcast.20, s32[2,32]{1,0:T(2,128)} %bitcast.21), custom_call_target="tpu_custom_call" | custom-call | tf_op jit(solution)/shard_map/pack_pages/pallas_call | solution.py:75
  3.0 0.0 copy-start.1
  3.0 52.3 %all-to-all-start = ((bf16[128,5,2,128]{3,2,1,0:T(2,128)(2,1)}), bf16[128,5,2,128]{3,2,1,0:T(2,128)(2,1)S(1)}, u32[]{:S(2)}, u32[]{:S(2)}) async-start(bf16[128,5,2,128]{3,2,1,0:T(2,128)(2,1)} %bitcast.5), calls=%async_computation | async-start | bytes 655360 | tf_op jit(solution)/shard_map/all_to_all | solution.py:280
  55.4 5.3 %collective-permute-start = (bf16[512,128]{1,0:T(8,128)(2,1)S(1)}, bf16[512,128]{1,0:T(8,128)(2,1)S(1)}, u32[]{:S(2)}, u32[]{:S(2)}) collective-permute-start(bf16[512,128]{1,0:T(8,128)(2,1)S(1)} %get-tuple-element.6.refs_3_), channel_id=1, source_target_pairs={{0,6},{2,8},{4,10},{6,12},{8,14},{10,16},{12,18},{14,20},{16,22},{... | collective-permute-start | bytes 393224 | tf_op jit(solution)/shard_map/ppermute | solution.py:32
  60.6 10.4 %collective-permute-start.1 = (bf16[512,128]{1,0:T(8,128)(2,1)S(1)}, bf16[512,128]{1,0:T(8,128)(2,1)S(1)}, u32[]{:S(2)}, u32[]{:S(2)}) collective-permute-start(bf16[512,128]{1,0:T(8,128)(2,1)S(1)} %get-tuple-element.6.refs_3_), channel_id=1, source_target_pairs={{0,12},{2,14},{4,16},{6,18},{8,20},{10,22},{12,24},{14,26},{16,28}... | collective-permute-start | bytes 393224 | tf_op jit(solution)/shard_map/ppermute | solution.py:32
  71.1 25.2 %collective-permute-done.refs_5_ = bf16[512,128]{1,0:T(8,128)(2,1)S(1)} collective-permute-done((bf16[512,128]{1,0:T(8,128)(2,1)S(1)}, bf16[512,128]{1,0:T(8,128)(2,1)S(1)}, u32[]{:S(2)}, u32[]{:S(2)}) %collective-permute-start) | collective-permute-done | bytes 131104 | tf_op jit(solution)/shard_map/ppermute | solution.py:32
  96.2 14.0 %collective-permute-done.1.refs_6_ = bf16[512,128]{1,0:T(8,128)(2,1)S(1)} collective-permute-done((bf16[512,128]{1,0:T(8,128)(2,1)S(1)}, bf16[512,128]{1,0:T(8,128)(2,1)S(1)}, u32[]{:S(2)}, u32[]{:S(2)}) %collective-permute-start.1) | collective-permute-done | bytes 131104 | tf_op jit(solution)/shard_map/ppermute | solution.py:32
  110.2 4.3 %collective-permute-start.2 = (bf16[1024,128]{1,0:T(8,128)(2,1)S(1)}, bf16[1024,128]{1,0:T(8,128)(2,1)S(1)}, u32[]{:S(2)}, u32[]{:S(2)}) collective-permute-start(bf16[1024,128]{1,0:T(8,128)(2,1)S(1)} %pad_maximum_fusion), channel_id=1, source_target_pairs={{0,2},{2,4},{4,6},{6,8},{8,10},{10,12},{12,14},{14,16},{16,18},{18... | collective-permute-start | bytes 786440 | tf_op jit(solution)/shard_map/ppermute | solution.py:32
  114.6 2.6 %collective-permute-start.4 = (bf16[512,128]{1,0:T(8,128)(2,1)S(1)}, bf16[512,128]{1,0:T(8,128)(2,1)S(1)}, u32[]{:S(2)}, u32[]{:S(2)}) collective-permute-start(bf16[512,128]{1,0:T(8,128)(2,1)S(1)} %get-tuple-element.6.refs_3_), channel_id=1, source_target_pairs={{0,2},{2,4},{4,6},{6,8},{8,10},{10,12},{12,14},{14,16},{16,18},{18... | collective-permute-start | bytes 393224 | tf_op jit(solution)/shard_map/ppermute | solution.py:32
  117.2 3.9 %collective-permute-done.2.refs_4_ = bf16[1024,128]{1,0:T(8,128)(2,1)S(1)} collective-permute-done((bf16[1024,128]{1,0:T(8,128)(2,1)S(1)}, bf16[1024,128]{1,0:T(8,128)(2,1)S(1)}, u32[]{:S(2)}, u32[]{:S(2)}) %collective-permute-start.2) | collective-permute-done | bytes 262176 | tf_op jit(solution)/shard_map/ppermute | solution.py:32
  121.1 4.2 %collective-permute-start.3 = (bf16[1024,128]{1,0:T(8,128)(2,1)S(1)}, bf16[1024,128]{1,0:T(8,128)(2,1)S(1)}, u32[]{:S(2)}, u32[]{:S(2)}) collective-permute-start(bf16[1024,128]{1,0:T(8,128)(2,1)S(1)} %collective-permute-done.2.refs_4_), channel_id=1, source_target_pairs={{0,2},{2,4},{4,6},{6,8},{8,10},{10,12},{12,14},{14,16},{16,18},{18... | collective-permute-start | bytes 786440 | tf_op jit(solution)/shard_map/ppermute | solution.py:32
  125.3 0.0 collective-permute-done.4.refs_4_
  125.3 2.2 %collective-permute-start.5 = (bf16[512,128]{1,0:T(8,128)(2,1)S(1)}, bf16[512,128]{1,0:T(8,128)(2,1)S(1)}, u32[]{:S(2)}, u32[]{:S(2)}) collective-permute-start(bf16[512,128]{1,0:T(8,128)(2,1)S(1)} %collective-permute-done.4.refs_4_), channel_id=1, source_target_pairs={{0,2},{2,4},{4,6},{6,8},{8,10},{10,12},{12,14},{14,16},{16,18},{18... | collective-permute-start | bytes 393224 | tf_op jit(solution)/shard_map/ppermute | solution.py:32
  127.6 0.0 copy-start
  127.6 1.2 copy-done
  128.8 5.8 %attend_part.2.refs_5_ = f32[6,144,640]{2,1,0:T(8,128)} custom-call(s32[1]{0:T(128)} %bitcast.refs_0_, s32[1,64]{1,0:T(1,128)} %bitcast.17, bf16[3,128,1280]{2,1,0:T(8,128)(2,1)S(1)} %bitcast.13, bf16[512,128]{1,0:T(8,128)(2,1)S(1)} %get-tuple-element.6.refs_3_, bf16[512,128]{1,0:T(8,128)(2,1)S(1)} %collective-permute-done.4.refs_4_, ...), custom_call_target="tpu_custom_call" | custom-call | tf_op jit(solution)/shard_map/attend_part/pallas_call | solution.py:257
  134.6 0.0 collective-permute-done.5.refs_3_
  134.6 0.0 copy-done.1
  134.6 5.7 %attend_part.3.refs_4_ = f32[6,144,640]{2,1,0:T(8,128)} custom-call(s32[1]{0:T(128)} %bitcast.refs_0_, s32[1,64]{1,0:T(1,128)} %bitcast.18, bf16[3,128,1280]{2,1,0:T(8,128)(2,1)S(1)} %bitcast.14, bf16[512,128]{1,0:T(8,128)(2,1)S(1)} %collective-permute-done.5.refs_3_, bf16[1024,128]{1,0:T(8,128)(2,1)S(1)} %collective-permute-done.2.refs_4_, ...), custom_call_target="tpu_custom_call" | custom-call | tf_op jit(solution)/shard_map/attend_part/pallas_call | solution.py:257
  140.3 0.0 collective-permute-done.3.refs_3_
  140.3 0.0 all-to-all-done
  140.3 6.1 %attend_last.1 = (bf16[3,128,1280]{2,1,0:T(8,128)(2,1)}, bf16[512,128]{1,0:T(8,128)(2,1)}) custom-call(s32[1]{0:T(128)} %bitcast.refs_0_, s32[1,64]{1,0:T(1,128)} %bitcast.19, bf16[3,128,1280]{2,1,0:T(8,128)(2,1)S(1)} %bitcast.15, bf16[1024,128]{1,0:T(8,128)(2,1)S(1)} %collective-permute-done.3.refs_3_, f32[6,144,640]{2,1,0:T(8,128)} %attend_part.3.refs_4_, ...), custom_call_target="tpu_custom_call" | custom-call | tf_op jit(solution)/shard_map/attend_last/pallas_call | solution.py:257
  (1 shorter events, 0.0 us)
Async XLA Ops:
  3.0 131.6 %copy-start.1 = (bf16[128,3,1280]{2,0,1:T(8,128)(2,1)S(1)}, bf16[128,3,1280]{2,0,1:T(8,128)(2,1)}, u32[]{:S(2)}) copy-start(bf16[128,3,1280]{2,0,1:T(8,128)(2,1)} %param.6) | copy-start | bytes 2949124
  3.0 137.3 %all-to-all-start = ((bf16[128,5,2,128]{3,2,1,0:T(2,128)(2,1)}), bf16[128,5,2,128]{3,2,1,0:T(2,128)(2,1)S(1)}, u32[]{:S(2)}, u32[]{:S(2)}) async-start(bf16[128,5,2,128]{3,2,1,0:T(2,128)(2,1)} %bitcast.5), calls=%async_computation | async-start | bytes 655360 | tf_op jit(solution)/shard_map/all_to_all | solution.py:280
  55.4 40.9 %collective-permute-start = (bf16[512,128]{1,0:T(8,128)(2,1)S(1)}, bf16[512,128]{1,0:T(8,128)(2,1)S(1)}, u32[]{:S(2)}, u32[]{:S(2)}) collective-permute-start(bf16[512,128]{1,0:T(8,128)(2,1)S(1)} %get-tuple-element.6.refs_3_), channel_id=1, source_target_pairs={{0,6},{2,8},{4,10},{6,12},{8,14},{10,16},{12,18},{14,20},{16,22},{... | collective-permute-start | bytes 393224 | tf_op jit(solution)/shard_map/ppermute | solution.py:32
  60.6 49.6 %collective-permute-start.1 = (bf16[512,128]{1,0:T(8,128)(2,1)S(1)}, bf16[512,128]{1,0:T(8,128)(2,1)S(1)}, u32[]{:S(2)}, u32[]{:S(2)}) collective-permute-start(bf16[512,128]{1,0:T(8,128)(2,1)S(1)} %get-tuple-element.6.refs_3_), channel_id=1, source_target_pairs={{0,12},{2,14},{4,16},{6,18},{8,20},{10,22},{12,24},{14,26},{16,28}... | collective-permute-start | bytes 393224 | tf_op jit(solution)/shard_map/ppermute | solution.py:32
  110.2 10.9 %collective-permute-start.2 = (bf16[1024,128]{1,0:T(8,128)(2,1)S(1)}, bf16[1024,128]{1,0:T(8,128)(2,1)S(1)}, u32[]{:S(2)}, u32[]{:S(2)}) collective-permute-start(bf16[1024,128]{1,0:T(8,128)(2,1)S(1)} %pad_maximum_fusion), channel_id=1, source_target_pairs={{0,2},{2,4},{4,6},{6,8},{8,10},{10,12},{12,14},{14,16},{16,18},{18... | collective-permute-start | bytes 786440 | tf_op jit(solution)/shard_map/ppermute | solution.py:32
  114.6 10.7 %collective-permute-start.4 = (bf16[512,128]{1,0:T(8,128)(2,1)S(1)}, bf16[512,128]{1,0:T(8,128)(2,1)S(1)}, u32[]{:S(2)}, u32[]{:S(2)}) collective-permute-start(bf16[512,128]{1,0:T(8,128)(2,1)S(1)} %get-tuple-element.6.refs_3_), channel_id=1, source_target_pairs={{0,2},{2,4},{4,6},{6,8},{8,10},{10,12},{12,14},{14,16},{16,18},{18... | collective-permute-start | bytes 393224 | tf_op jit(solution)/shard_map/ppermute | solution.py:32
  121.1 19.1 %collective-permute-start.3 = (bf16[1024,128]{1,0:T(8,128)(2,1)S(1)}, bf16[1024,128]{1,0:T(8,128)(2,1)S(1)}, u32[]{:S(2)}, u32[]{:S(2)}) collective-permute-start(bf16[1024,128]{1,0:T(8,128)(2,1)S(1)} %collective-permute-done.2.refs_4_), channel_id=1, source_target_pairs={{0,2},{2,4},{4,6},{6,8},{8,10},{10,12},{12,14},{14,16},{16,18},{18... | collective-permute-start | bytes 786440 | tf_op jit(solution)/shard_map/ppermute | solution.py:32
  125.3 9.2 %collective-permute-start.5 = (bf16[512,128]{1,0:T(8,128)(2,1)S(1)}, bf16[512,128]{1,0:T(8,128)(2,1)S(1)}, u32[]{:S(2)}, u32[]{:S(2)}) collective-permute-start(bf16[512,128]{1,0:T(8,128)(2,1)S(1)} %collective-permute-done.4.refs_4_), channel_id=1, source_target_pairs={{0,2},{2,4},{4,6},{6,8},{8,10},{10,12},{12,14},{14,16},{16,18},{18... | collective-permute-start | bytes 393224 | tf_op jit(solution)/shard_map/ppermute | solution.py:32
  127.6 1.2 copy-start

commit v2 on v0

--- a/solution.py
+++ b/solution.py
@@ -110,7 +110,7 @@
         place_kernel,
         out_shape=jax.ShapeDtypeStruct((slots * PAGE * 2, HD), BF16),
         name="place_pages",
-    )(near_core(got))
+    )(got)
 
 
 def attend_kernel(groups, first, final, *refs):
@@ -119,29 +119,23 @@
     arrays = 1 + max(g[0] for g in groups)
     kv = refs[3 : 3 + arrays]
     rest = refs[3 + arrays :]
-    state_in = None if first else rest.pop(0)
-    result_ref = rest.pop(0)
-    work, sems = rest[:2]
-    staged = rest[2] if final else None
+    if not first:
+        acc_in, stats_in = rest[:2]
+        rest = rest[2:]
+    if final:
+        result_ref, sems, staged = rest
+    else:
+        acc_ref, stats_ref = rest
     layers, rows, width = q_ref.shape
     wide = QPER * HD
     units = layers * width // wide
     reqs = lens_ref.shape[1]
 
-    def fetch(i):
-        return pltpu.make_async_copy(state_in.at[i], work.at[i], sems.at[0, i])
-
     def send(i):
-        if not final:
-            return pltpu.make_async_copy(work.at[i], result_ref.at[i], sems.at[1, i])
         lanes = pl.ds(pl.multiple_of(i % (width // wide) * wide, HD), wide)
         return pltpu.make_async_copy(
-            staged.at[i], result_ref.at[i // (width // wide), :, lanes], sems.at[1, i]
+            staged.at[i], result_ref.at[i // (width // wide), :, lanes], sems.at[i]
         )
-
-    if not first:
-        for i in range(units):
-            fetch(i).start()
 
     base = mine_ref[0] * rows
     lens = jnp.broadcast_to(lens_ref[...], (reqs, reqs)).astype(F32)
@@ -158,8 +152,8 @@
         head = i % (width // wide)
         layer = i // (width // wide)
         if not first:
-            old = work[i, HD : HD + 1]
-            old_total = work[i, HD + 8 : HD + 9]
+            old = stats_in[i, 0:1]
+            old_total = stats_in[i, 8:9]
         if some:
             key_i = lax.broadcasted_iota(jnp.int32, (rows, rows), 0)
             qry_i = lax.broadcasted_iota(jnp.int32, (rows, rows), 1)
@@ -185,17 +179,20 @@
             if not first:
                 shrink = jnp.exp2(old - top)
                 total += old_total * shrink
-                acc += work[i, :HD] * shrink
+                acc += acc_in[i].astype(F32) * shrink
         if final:
             if not some:
-                total, acc = old_total, work[i, :HD]
+                total, acc = old_total, acc_in[i].astype(F32)
             normed = (acc * (1.0 / total)).astype(BF16)
             for q in range(QPER):
                 staged[i, :, q * HD : (q + 1) * HD] = normed[:, q * rows : (q + 1) * rows].T
         elif some:
-            work[i, :HD] = acc
-            work[i, HD : HD + 8] = jnp.broadcast_to(top, (8, wide))
-            work[i, HD + 8 :] = jnp.broadcast_to(total, (8, wide))
+            acc_ref[i] = acc.astype(BF16)
+            stats_ref[i, :8] = jnp.broadcast_to(top, (8, wide))
+            stats_ref[i, 8:] = jnp.broadcast_to(total, (8, wide))
+        else:
+            acc_ref[i] = acc_in[i]
+            stats_ref[i] = stats_in[i]
 
     for used in range(1 if first else 0, len(groups) + 1):
         some = groups[:used]
@@ -210,15 +207,14 @@
             @pl.loop(0, units, step=PAIR)
             def _(i):
                 for j in range(PAIR):
-                    if not first:
-                        fetch(i + j).wait()
-                for j in range(PAIR):
                     take(some, i + j)
-                for j in range(PAIR):
-                    send(i + j).start()
-
-    for i in range(units):
-        send(i).wait()
+                if final:
+                    for j in range(PAIR):
+                        send(i + j).start()
+
+    if final:
+        for i in range(units):
+            send(i).wait()
 
 
 def attend(mine, lengths, queries, arrays, groups, state, final):
@@ -231,17 +227,23 @@
         pl.BlockSpec(memory_space=pltpu.VMEM),
     ]
     in_specs += [pl.BlockSpec(memory_space=pltpu.VMEM) for _ in arrays]
-    kept = (units, HD + 16, QPER * rows)
+    kept = ((units, HD, QPER * rows), BF16), ((units, 16, QPER * rows), F32)
     operands = [mine, lengths, near_core(queries), *map(near_core, arrays)]
     if not first:
-        in_specs.append(pl.BlockSpec(memory_space=pl.ANY))
-        operands.append(state)
-    scratch = [pltpu.VMEM(kept, F32), pltpu.SemaphoreType.DMA((2, units))]
+        in_specs += [pl.BlockSpec(memory_space=pltpu.VMEM)] * 2
+        operands += map(near_core, state)
     if final:
-        scratch.append(pltpu.VMEM((units, rows, QPER * HD), BF16))
         out_shape = jax.ShapeDtypeStruct(queries.shape, BF16)
+        out_specs = pl.BlockSpec(memory_space=pl.ANY)
+        scratch = [
+            pltpu.SemaphoreType.DMA((units,)),
+            pltpu.VMEM((units, rows, QPER * HD), BF16),
+        ]
     else:
-        out_shape = jax.ShapeDtypeStruct(kept, F32)
+        out_shape = tuple(pltpu.VMEM(*k) for k in kept)
+        out_specs = (pl.BlockSpec(memory_space=pltpu.VMEM),) * 2
+        scratch = []
+    aliases = {} if first or final else {len(operands) - 2: 0, len(operands) - 1: 1}
 
     def kernel(*refs):
         attend_kernel(groups, first, final, *refs)
@@ -249,9 +251,10 @@
     return pl.pallas_call(
         kernel,
         in_specs=in_specs,
-        out_specs=pl.BlockSpec(memory_space=pl.ANY),
+        out_specs=out_specs,
         out_shape=out_shape,
         scratch_shapes=scratch,
+        input_output_aliases=aliases,
         name="attend_last" if final else "attend_part",
     )(*operands)
 

time: 148 us -> 150 us (1.014)
  local copies, waits for them, and re-layouts: 1.2 us -> 4.9 us
  Pallas kernels: 20.9 us -> 18.4 us
    unnamed x4 -> x12, local copies, waits for them, and re-layouts: 1.2 us -> 4.9 us
    pallas_call x3, Pallas kernels: 16.6 us -> 13.1 us  [attend(): pl.pallas_call(kernel, in_specs=in_specs, out_specs=out_specs, out_shape=...]
  transfers between devices with their start and end apart: 7 -> 7, of which waited for: 3 -> 4; matrix products, arithmetic and copies ran while one was open for 0% -> 0% of each run, Pallas kernels for 11% -> 9%
where the time goes in v2:
time: 150 us
  starting transfers between devices  81.7 us (54%)
  waiting for transfers between devices  43.7 us (29%)
  Pallas kernels  18.4 us (12%)
  local copies, waits for them, and re-layouts  4.9 us (3%)
    all_to_all x1, starting transfers between devices, shards(): lax.all_to_all(outgoing.reshape(seq_count, CHUNKS, 2, HD), 'seq', split_a...  52.4 us
    ppermute x6, waiting for transfers between devices, shifted(): return lax.ppermute(x, 'seq', pairs)  43.7 us
    ppermute x6, starting transfers between devices, shifted(): return lax.ppermute(x, 'seq', pairs)  29.4 us
    pallas_call x3, Pallas kernels, attend(): pl.pallas_call(kernel, in_specs=in_specs, out_specs=out_specs, out_shape=...  13.1 us
    unnamed x12, local copies, waits for them, and re-layouts  4.9 us
  transfers between devices with their start and end apart: 7, of which 4 were waited for; matrix products, arithmetic and copies ran while one was open for 0% of the time, Pallas kernels for 9%

profile of v2, /device:TPU:46, one launch (start us, length us, event | category | flops | bytes accessed | tf_op | source)
XLA Modules:
  0.0 149.5 jit_solution(10239041408146623518)
XLA Ops:
  0.6 2.4 %pack_pages.1 = (bf16[512,128]{1,0:T(8,128)(2,1)S(1)}, bf16[1280,128]{1,0:T(8,128)(2,1)}) custom-call(bf16[128,256]{1,0:T(8,128)(2,1)} %keys_ref.1, bf16[128,256]{1,0:T(8,128)(2,1)} %vals_ref.1, s32[2,32]{1,0:T(2,128)} %bitcast.21, s32[2,32]{1,0:T(2,128)} %bitcast.22), custom_call_target="tpu_custom_call" | custom-call | tf_op jit(solution)/shard_map/pack_pages/pallas_call | solution.py:75
  3.0 0.0 copy-start
  3.0 52.4 %all-to-all-start = ((bf16[128,5,2,128]{3,2,1,0:T(2,128)(2,1)}), bf16[128,5,2,128]{3,2,1,0:T(2,128)(2,1)}, u32[]{:S(2)}, u32[]{:S(2)}) async-start(bf16[128,5,2,128]{3,2,1,0:T(2,128)(2,1)} %bitcast.6), calls=%async_computation | async-start | bytes 655360 | tf_op jit(solution)/shard_map/all_to_all | solution.py:275
  55.4 5.3 %collective-permute-start = (bf16[512,128]{1,0:T(8,128)(2,1)S(1)}, bf16[512,128]{1,0:T(8,128)(2,1)S(1)}, u32[]{:S(2)}, u32[]{:S(2)}) collective-permute-start(bf16[512,128]{1,0:T(8,128)(2,1)S(1)} %get-tuple-element.8.refs_3_), channel_id=1, source_target_pairs={{0,6},{2,8},{4,10},{6,12},{8,14},{10,16},{12,18},{14,20},{16,22},{... | collective-permute-start | bytes 393224 | tf_op jit(solution)/shard_map/ppermute | solution.py:32
  60.7 10.4 %collective-permute-start.1 = (bf16[512,128]{1,0:T(8,128)(2,1)S(1)}, bf16[512,128]{1,0:T(8,128)(2,1)S(1)}, u32[]{:S(2)}, u32[]{:S(2)}) collective-permute-start(bf16[512,128]{1,0:T(8,128)(2,1)S(1)} %get-tuple-element.8.refs_3_), channel_id=1, source_target_pairs={{0,12},{2,14},{4,16},{6,18},{8,20},{10,22},{12,24},{14,26},{16,28}... | collective-permute-start | bytes 393224 | tf_op jit(solution)/shard_map/ppermute | solution.py:32
  71.1 25.1 %collective-permute-done.refs_5_ = bf16[512,128]{1,0:T(8,128)(2,1)S(1)} collective-permute-done((bf16[512,128]{1,0:T(8,128)(2,1)S(1)}, bf16[512,128]{1,0:T(8,128)(2,1)S(1)}, u32[]{:S(2)}, u32[]{:S(2)}) %collective-permute-start) | collective-permute-done | bytes 131104 | tf_op jit(solution)/shard_map/ppermute | solution.py:32
  96.3 14.0 %collective-permute-done.1.refs_6_ = bf16[512,128]{1,0:T(8,128)(2,1)S(1)} collective-permute-done((bf16[512,128]{1,0:T(8,128)(2,1)S(1)}, bf16[512,128]{1,0:T(8,128)(2,1)S(1)}, u32[]{:S(2)}, u32[]{:S(2)}) %collective-permute-start.1) | collective-permute-done | bytes 131104 | tf_op jit(solution)/shard_map/ppermute | solution.py:32
  110.3 4.3 %collective-permute-start.2 = (bf16[1024,128]{1,0:T(8,128)(2,1)S(1)}, bf16[1024,128]{1,0:T(8,128)(2,1)S(1)}, u32[]{:S(2)}, u32[]{:S(2)}) collective-permute-start(bf16[1024,128]{1,0:T(8,128)(2,1)S(1)} %pad_maximum_fusion), channel_id=1, source_target_pairs={{0,2},{2,4},{4,6},{6,8},{8,10},{10,12},{12,14},{14,16},{16,18},{18... | collective-permute-start | bytes 786440 | tf_op jit(solution)/shard_map/ppermute | solution.py:32
  114.6 3.0 %collective-permute-start.4 = (bf16[512,128]{1,0:T(8,128)(2,1)S(1)}, bf16[512,128]{1,0:T(8,128)(2,1)S(1)}, u32[]{:S(2)}, u32[]{:S(2)}) collective-permute-start(bf16[512,128]{1,0:T(8,128)(2,1)S(1)} %get-tuple-element.8.refs_3_), channel_id=1, source_target_pairs={{0,2},{2,4},{4,6},{6,8},{8,10},{10,12},{12,14},{14,16},{16,18},{18... | collective-permute-start | bytes 393224 | tf_op jit(solution)/shard_map/ppermute | solution.py:32
  117.6 3.6 %collective-permute-done.2.refs_4_ = bf16[1024,128]{1,0:T(8,128)(2,1)S(1)} collective-permute-done((bf16[1024,128]{1,0:T(8,128)(2,1)S(1)}, bf16[1024,128]{1,0:T(8,128)(2,1)S(1)}, u32[]{:S(2)}, u32[]{:S(2)}) %collective-permute-start.2) | collective-permute-done | bytes 262176 | tf_op jit(solution)/shard_map/ppermute | solution.py:32
  121.2 4.1 %collective-permute-start.3 = (bf16[1024,128]{1,0:T(8,128)(2,1)S(1)}, bf16[1024,128]{1,0:T(8,128)(2,1)S(1)}, u32[]{:S(2)}, u32[]{:S(2)}) collective-permute-start(bf16[1024,128]{1,0:T(8,128)(2,1)S(1)} %collective-permute-done.2.refs_4_), channel_id=1, source_target_pairs={{0,2},{2,4},{4,6},{6,8},{8,10},{10,12},{12,14},{14,16},{16,18},{18... | collective-permute-start | bytes 786440 | tf_op jit(solution)/shard_map/ppermute | solution.py:32
  125.3 0.0 collective-permute-done.4.refs_4_
  125.3 2.2 %collective-permute-start.5 = (bf16[512,128]{1,0:T(8,128)(2,1)S(1)}, bf16[512,128]{1,0:T(8,128)(2,1)S(1)}, u32[]{:S(2)}, u32[]{:S(2)}) collective-permute-start(bf16[512,128]{1,0:T(8,128)(2,1)S(1)} %collective-permute-done.4.refs_4_), channel_id=1, source_target_pairs={{0,2},{2,4},{4,6},{6,8},{8,10},{10,12},{12,14},{14,16},{16,18},{18... | collective-permute-start | bytes 393224 | tf_op jit(solution)/shard_map/ppermute | solution.py:32
  127.6 0.0 copy-done
  127.6 4.8 %attend_part.2 = (bf16[6,128,640]{2,1,0:T(8,128)(2,1)S(1)}, f32[6,16,640]{2,1,0:T(8,128)S(1)}) custom-call(s32[1]{0:T(128)} %bitcast.refs_0_, s32[1,64]{1,0:T(1,128)} %bitcast.18, bf16[3,128,1280]{2,1,0:T(8,128)(2,1)S(1)} %bitcast.13, bf16[512,128]{1,0:T(8,128)(2,1)S(1)} %get-tuple-element.8.refs_3_, bf16[512,128]{1,0:T(8,128)(2,1)S(1)} %collective-permute-done.4.refs_4_, ...), custom_call_target="tpu_custom_call" | custom-call | tf_op jit(solution)/shard_map/attend_part/pallas_call | solution.py:251
  132.4 0.0 copy-start.2
  132.4 0.9 copy-done.2
  133.4 1.0 collective-permute-done.5.refs_3_
  134.3 0.0 copy-start.4
  134.3 0.7 copy-done.4
  135.0 0.0 copy-start.1
  135.0 1.2 copy-done.1
  136.2 0.0 copy-start.3
  136.2 1.2 copy-done.3
  137.4 0.0 copy-start.5
  137.4 0.9 copy-done.5
  138.3 4.0 %attend_part.3 = (bf16[6,128,640]{2,1,0:T(8,128)(2,1)S(1)}, f32[6,16,640]{2,1,0:T(8,128)S(1)}) custom-call(s32[1]{0:T(128)} %bitcast.refs_0_, s32[1,64]{1,0:T(1,128)} %bitcast.19, bf16[3,128,1280]{2,1,0:T(8,128)(2,1)S(1)} %bitcast.14, bf16[512,128]{1,0:T(8,128)(2,1)S(1)} %copy-done.5, ...), custom_call_target="tpu_custom_call", output_to_operand_aliasing={{0}: (5, {}), {1}: (6, {})} | custom-call | tf_op jit(solution)/shard_map/attend_part/pallas_call | solution.py:251
  142.3 0.0 collective-permute-done.3.refs_3_
  142.3 4.3 %attend_last.1 = bf16[3,128,1280]{2,1,0:T(8,128)(2,1)} custom-call(s32[1]{0:T(128)} %bitcast.refs_0_, s32[1,64]{1,0:T(1,128)} %bitcast.20, bf16[3,128,1280]{2,1,0:T(8,128)(2,1)S(1)} %bitcast.15, bf16[1024,128]{1,0:T(8,128)(2,1)S(1)} %collective-permute-done.3.refs_3_, bf16[6,128,640]{2,1,0:T(8,128)(2,1)S(1)} %get-tuple-element.11.refs_4_, ...), custom_call_target="tpu_custom_call" | custom-call | tf_op jit(solution)/shard_map/attend_last/pallas_call | solution.py:251
  146.6 0.0 all-to-all-done
  146.6 2.9 %place_pages.1 = bf16[512,128]{1,0:T(8,128)(2,1)} custom-call(bf16[1280,128]{1,0:T(8,128)(2,1)} %bitcast.7.got_ref), custom_call_target="tpu_custom_call" | custom-call | tf_op jit(solution)/shard_map/place_pages/pallas_call | solution.py:109
  (1 shorter events, 0.0 us)
Async XLA Ops:
  3.0 124.6 %copy-start = (bf16[128,3,1280]{2,0,1:T(8,128)(2,1)S(1)}, bf16[128,3,1280]{2,0,1:T(8,128)(2,1)}, u32[]{:S(2)}) copy-start(bf16[128,3,1280]{2,0,1:T(8,128)(2,1)} %param.6) | copy-start | bytes 2949124
  3.0 143.6 %all-to-all-start = ((bf16[128,5,2,128]{3,2,1,0:T(2,128)(2,1)}), bf16[128,5,2,128]{3,2,1,0:T(2,128)(2,1)}, u32[]{:S(2)}, u32[]{:S(2)}) async-start(bf16[128,5,2,128]{3,2,1,0:T(2,128)(2,1)} %bitcast.6), calls=%async_computation | async-start | bytes 655360 | tf_op jit(solution)/shard_map/all_to_all | solution.py:275
  55.4 40.9 %collective-permute-start = (bf16[512,128]{1,0:T(8,128)(2,1)S(1)}, bf16[512,128]{1,0:T(8,128)(2,1)S(1)}, u32[]{:S(2)}, u32[]{:S(2)}) collective-permute-start(bf16[512,128]{1,0:T(8,128)(2,1)S(1)} %get-tuple-element.8.refs_3_), channel_id=1, source_target_pairs={{0,6},{2,8},{4,10},{6,12},{8,14},{10,16},{12,18},{14,20},{16,22},{... | collective-permute-start | bytes 393224 | tf_op jit(solution)/shard_map/ppermute | solution.py:32
  60.7 49.6 %collective-permute-start.1 = (bf16[512,128]{1,0:T(8,128)(2,1)S(1)}, bf16[512,128]{1,0:T(8,128)(2,1)S(1)}, u32[]{:S(2)}, u32[]{:S(2)}) collective-permute-start(bf16[512,128]{1,0:T(8,128)(2,1)S(1)} %get-tuple-element.8.refs_3_), channel_id=1, source_target_pairs={{0,12},{2,14},{4,16},{6,18},{8,20},{10,22},{12,24},{14,26},{16,28}... | collective-permute-start | bytes 393224 | tf_op jit(solution)/shard_map/ppermute | solution.py:32
  110.3 10.9 %collective-permute-start.2 = (bf16[1024,128]{1,0:T(8,128)(2,1)S(1)}, bf16[1024,128]{1,0:T(8,128)(2,1)S(1)}, u32[]{:S(2)}, u32[]{:S(2)}) collective-permute-start(bf16[1024,128]{1,0:T(8,128)(2,1)S(1)} %pad_maximum_fusion), channel_id=1, source_target_pairs={{0,2},{2,4},{4,6},{6,8},{8,10},{10,12},{12,14},{14,16},{16,18},{18... | collective-permute-start | bytes 786440 | tf_op jit(solution)/shard_map/ppermute | solution.py:32
  114.6 10.7 %collective-permute-start.4 = (bf16[512,128]{1,0:T(8,128)(2,1)S(1)}, bf16[512,128]{1,0:T(8,128)(2,1)S(1)}, u32[]{:S(2)}, u32[]{:S(2)}) collective-permute-start(bf16[512,128]{1,0:T(8,128)(2,1)S(1)} %get-tuple-element.8.refs_3_), channel_id=1, source_target_pairs={{0,2},{2,4},{4,6},{6,8},{8,10},{10,12},{12,14},{14,16},{16,18},{18... | collective-permute-start | bytes 393224 | tf_op jit(solution)/shard_map/ppermute | solution.py:32
  121.2 21.1 %collective-permute-start.3 = (bf16[1024,128]{1,0:T(8,128)(2,1)S(1)}, bf16[1024,128]{1,0:T(8,128)(2,1)S(1)}, u32[]{:S(2)}, u32[]{:S(2)}) collective-permute-start(bf16[1024,128]{1,0:T(8,128)(2,1)S(1)} %collective-permute-done.2.refs_4_), channel_id=1, source_target_pairs={{0,2},{2,4},{4,6},{6,8},{8,10},{10,12},{12,14},{14,16},{16,18},{18... | collective-permute-start | bytes 786440 | tf_op jit(solution)/shard_map/ppermute | solution.py:32
  125.3 9.0 %collective-permute-start.5 = (bf16[512,128]{1,0:T(8,128)(2,1)S(1)}, bf16[512,128]{1,0:T(8,128)(2,1)S(1)}, u32[]{:S(2)}, u32[]{:S(2)}) collective-permute-start(bf16[512,128]{1,0:T(8,128)(2,1)S(1)} %collective-permute-done.4.refs_4_), channel_id=1, source_target_pairs={{0,2},{2,4},{4,6},{6,8},{8,10},{10,12},{12,14},{14,16},{16,18},{18... | collective-permute-start | bytes 393224 | tf_op jit(solution)/shard_map/ppermute | solution.py:32
  132.4 0.9 copy-start.2
  134.3 0.7 copy-start.4
  135.0 1.2 copy-start.1
  136.2 1.2 copy-start.3
  137.4 0.9 copy-start.5

commit v3 on v0

--- a/solution.py
+++ b/solution.py
@@ -38,8 +38,8 @@
 
 def pack_kernel(keys_ref, vals_ref, owner_ref, slot_ref, own_ref, out_ref):
     for c in range(2):
-        own_ref[c * HD : (c + 1) * HD] = keys_ref[:, c * HD : (c + 1) * HD]
-        own_ref[(2 + c) * HD : (3 + c) * HD] = vals_ref[:, c * HD : (c + 1) * HD].T
+        own_ref[c] = keys_ref[:, c * HD : (c + 1) * HD]
+        own_ref[2 + c] = vals_ref[:, c * HD : (c + 1) * HD].T
     rows = keys_ref.shape[0]
     pages = rows // PAGE
     per = CHUNKS * 2
@@ -60,7 +60,7 @@
     parts = []
     for c in range(2):
         parts += [keys_ref[:, c * HD : (c + 1) * HD], vals_ref[:, c * HD : (c + 1) * HD]]
-    step = 2 * HD
+    step = 5 * HD
     for begin in range(0, total, step):
         row = begin + lax.broadcasted_iota(jnp.int32, (step, rows), 0)
         acc = jnp.zeros((step, HD), F32)
@@ -75,7 +75,7 @@
     return pl.pallas_call(
         pack_kernel,
         out_shape=(
-            pltpu.VMEM((4 * HD, keys.shape[0]), BF16),
+            pltpu.VMEM((4, HD, keys.shape[0]), BF16),
             pltpu.VMEM((seq_count * CHUNKS * 2, HD), BF16),
         ),
         name="pack_pages",
@@ -165,9 +165,9 @@
             qry_i = lax.broadcasted_iota(jnp.int32, (rows, rows), 1)
             keys, vals, masks = [], [], []
             for source, index, distance in some:
-                at = pl.multiple_of((4 * index + head) * HD, HD)
-                keys.append(kv[source][pl.ds(at, HD)])
-                vals.append(kv[source][pl.ds(at + 2 * HD, HD)])
+                ref = kv[source]
+                keys.append(ref[head] if index is None else ref[index, head])
+                vals.append(ref[2 + head] if index is None else ref[index, 2 + head])
                 inside = key_i >= begin + distance * rows
                 masks.append(inside & (key_i <= qry_i) if distance == 0 else inside)
             v_all = jnp.concatenate(vals, axis=1)
@@ -273,12 +273,12 @@
         outgoing.reshape(seq_count, CHUNKS, 2, HD), "seq", split_axis=0, concat_axis=0, tiled=True
     )
 
-    b47 = shifted(jnp.concatenate([b3, b6]), 1)
+    b47 = shifted(jnp.stack([b3, b6]), 1)
     b2 = shifted(b1, 1)
-    groups = [(0, 0, 0), (1, 0, 1), (2, 0, 3), (3, 0, 6)]
+    groups = [(0, None, 0), (1, None, 1), (2, None, 3), (3, None, 6)]
     state = attend(mine, lens, flat_q, [own, b1, b3, b6], groups, None, False)
     b58 = shifted(b47, 1)
-    groups = [(0, 0, 2), (1, 0, 4), (1, 1, 7)]
+    groups = [(0, None, 2), (1, 0, 4), (1, 1, 7)]
     state = attend(mine, lens, flat_q, [b2, b47], groups, state, False)
     out = attend(mine, lens, flat_q, [b58], [(0, 0, 5), (0, 1, 8)], state, True)
     attended = out.transpose(1, 0, 2)

time: 148 us -> 148 us (level)
  no operation moved by 1% of the time
where the time goes in v3:
time: 148 us; the launch traced here: 147 us
  starting transfers between devices  81.4 us (55%)
  waiting for transfers between devices  43.1 us (29%)
  Pallas kernels  20.9 us (14%)
    all_to_all x1, starting transfers between devices, shards(): lax.all_to_all(outgoing.reshape(seq_count, CHUNKS, 2, HD), 'seq', split_a...  52.3 us
    ppermute x6, waiting for transfers between devices, shifted(): return lax.ppermute(x, 'seq', pairs)  43.1 us
    ppermute x6, starting transfers between devices, shifted(): return lax.ppermute(x, 'seq', pairs)  29.1 us
    pallas_call x3, Pallas kernels, attend(): pl.pallas_call(kernel, in_specs=in_specs, out_specs=pl.BlockSpec(memory_s...  16.6 us
  transfers between devices with their start and end apart: 7, of which 3 were waited for; matrix products, arithmetic and copies ran while one was open for 0% of the time, Pallas kernels for 11%

profile of v3, /device:TPU:46, one launch (start us, length us, event | category | flops | bytes accessed | tf_op | source)
XLA Modules:
  0.0 147.4 jit_solution(11408751535454675839)
XLA Ops:
  0.6 2.4 %pack_pages.1 = (bf16[4,128,128]{2,1,0:T(8,128)(2,1)S(1)}, bf16[1280,128]{1,0:T(8,128)(2,1)}) custom-call(bf16[128,256]{1,0:T(8,128)(2,1)} %keys_ref.1, bf16[128,256]{1,0:T(8,128)(2,1)} %vals_ref.1, s32[2,32]{1,0:T(2,128)} %bitcast.26, s32[2,32]{1,0:T(2,128)} %bitcast.27), custom_call_target="tpu_custom_call" | custom-call | tf_op jit(solution)/shard_map/pack_pages/pallas_call | solution.py:75
  3.0 0.0 copy-start.1
  3.0 52.3 %all-to-all-start = ((bf16[128,5,2,128]{3,2,1,0:T(2,128)(2,1)}), bf16[128,5,2,128]{3,2,1,0:T(2,128)(2,1)S(1)}, u32[]{:S(2)}, u32[]{:S(2)}) async-start(bf16[128,5,2,128]{3,2,1,0:T(2,128)(2,1)} %bitcast.8), calls=%async_computation | async-start | bytes 655360 | tf_op jit(solution)/shard_map/all_to_all | solution.py:272
  55.3 5.3 %collective-permute-start = (bf16[4,128,128]{2,1,0:T(8,128)(2,1)S(1)}, bf16[4,128,128]{2,1,0:T(8,128)(2,1)S(1)}, u32[]{:S(2)}, u32[]{:S(2)}) collective-permute-start(bf16[4,128,128]{2,1,0:T(8,128)(2,1)S(1)} %get-tuple-element.4.refs_3_), channel_id=1, source_target_pairs={{0,6},{2,8},{4,10},{6,12},{8,14},{10,16},{12,18},{14,20},{16,22},{... | collective-permute-start | bytes 393224 | tf_op jit(solution)/shard_map/ppermute | solution.py:32
  60.6 10.4 %collective-permute-start.1 = (bf16[4,128,128]{2,1,0:T(8,128)(2,1)S(1)}, bf16[4,128,128]{2,1,0:T(8,128)(2,1)S(1)}, u32[]{:S(2)}, u32[]{:S(2)}) collective-permute-start(bf16[4,128,128]{2,1,0:T(8,128)(2,1)S(1)} %get-tuple-element.4.refs_3_), channel_id=1, source_target_pairs={{0,12},{2,14},{4,16},{6,18},{8,20},{10,22},{12,24},{14,26},{16,28}... | collective-permute-start | bytes 393224 | tf_op jit(solution)/shard_map/ppermute | solution.py:32
  71.1 25.2 %collective-permute-done.refs_5_ = bf16[4,128,128]{2,1,0:T(8,128)(2,1)S(1)} collective-permute-done((bf16[4,128,128]{2,1,0:T(8,128)(2,1)S(1)}, bf16[4,128,128]{2,1,0:T(8,128)(2,1)S(1)}, u32[]{:S(2)}, u32[]{:S(2)}) %collective-permute-start) | collective-permute-done | bytes 131104 | tf_op jit(solution)/shard_map/ppermute | solution.py:32
  96.2 14.0 %collective-permute-done.1.refs_6_ = bf16[4,128,128]{2,1,0:T(8,128)(2,1)S(1)} collective-permute-done((bf16[4,128,128]{2,1,0:T(8,128)(2,1)S(1)}, bf16[4,128,128]{2,1,0:T(8,128)(2,1)S(1)}, u32[]{:S(2)}, u32[]{:S(2)}) %collective-permute-start.1) | collective-permute-done | bytes 131104 | tf_op jit(solution)/shard_map/ppermute | solution.py:32
  110.2 4.3 %collective-permute-start.2 = (bf16[2,4,128,128]{3,2,1,0:T(8,128)(2,1)S(1)}, bf16[2,4,128,128]{3,2,1,0:T(8,128)(2,1)S(1)}, u32[]{:S(2)}, u32[]{:S(2)}) collective-permute-start(bf16[2,4,128,128]{3,2,1,0:T(8,128)(2,1)S(1)} %pad_maximum_fusion), channel_id=1, source_target_pairs={{0,2},{2,4},{4,6},{6,8},{8,10},{10,12},{12,14},{14,16},{16,18},{18... | collective-permute-start | bytes 786440 | tf_op jit(solution)/shard_map/ppermute | solution.py:32
  114.6 2.6 %collective-permute-start.4 = (bf16[4,128,128]{2,1,0:T(8,128)(2,1)S(1)}, bf16[4,128,128]{2,1,0:T(8,128)(2,1)S(1)}, u32[]{:S(2)}, u32[]{:S(2)}) collective-permute-start(bf16[4,128,128]{2,1,0:T(8,128)(2,1)S(1)} %get-tuple-element.4.refs_3_), channel_id=1, source_target_pairs={{0,2},{2,4},{4,6},{6,8},{8,10},{10,12},{12,14},{14,16},{16,18},{18... | collective-permute-start | bytes 393224 | tf_op jit(solution)/shard_map/ppermute | solution.py:32
  117.2 3.9 %collective-permute-done.2.refs_4_ = bf16[2,4,128,128]{3,2,1,0:T(8,128)(2,1)S(1)} collective-permute-done((bf16[2,4,128,128]{3,2,1,0:T(8,128)(2,1)S(1)}, bf16[2,4,128,128]{3,2,1,0:T(8,128)(2,1)S(1)}, u32[]{:S(2)}, u32[]{:S(2)}) %collective-permute-start.2) | collective-permute-done | bytes 262176 | tf_op jit(solution)/shard_map/ppermute | solution.py:32
  121.1 4.2 %collective-permute-start.3 = (bf16[2,4,128,128]{3,2,1,0:T(8,128)(2,1)S(1)}, bf16[2,4,128,128]{3,2,1,0:T(8,128)(2,1)S(1)}, u32[]{:S(2)}, u32[]{:S(2)}) collective-permute-start(bf16[2,4,128,128]{3,2,1,0:T(8,128)(2,1)S(1)} %collective-permute-done.2.refs_4_), channel_id=1, source_target_pairs={{0,2},{2,4},{4,6},{6,8},{8,10},{10,12},{12,14},{14,16},{16,18},{18... | collective-permute-start | bytes 786440 | tf_op jit(solution)/shard_map/ppermute | solution.py:32
  125.3 0.0 collective-permute-done.4.refs_4_
  125.3 2.2 %collective-permute-start.5 = (bf16[4,128,128]{2,1,0:T(8,128)(2,1)S(1)}, bf16[4,128,128]{2,1,0:T(8,128)(2,1)S(1)}, u32[]{:S(2)}, u32[]{:S(2)}) collective-permute-start(bf16[4,128,128]{2,1,0:T(8,128)(2,1)S(1)} %collective-permute-done.4.refs_4_), channel_id=1, source_target_pairs={{0,2},{2,4},{4,6},{6,8},{8,10},{10,12},{12,14},{14,16},{16,18},{18... | collective-permute-start | bytes 393224 | tf_op jit(solution)/shard_map/ppermute | solution.py:32
  127.6 0.0 copy-start
  127.6 1.2 copy-done
  128.8 5.8 %attend_part.2.refs_5_ = f32[6,144,640]{2,1,0:T(8,128)} custom-call(s32[1]{0:T(128)} %bitcast.refs_0_, s32[1,64]{1,0:T(1,128)} %bitcast.23, bf16[3,128,1280]{2,1,0:T(8,128)(2,1)S(1)} %bitcast.15, bf16[4,128,128]{2,1,0:T(8,128)(2,1)S(1)} %get-tuple-element.4.refs_3_, bf16[4,128,128]{2,1,0:T(8,128)(2,1)S(1)} %collective-permute-done.4.refs_4_, ...), custom_call_target="tpu_custom_call" | custom-call | tf_op jit(solution)/shard_map/attend_part/pallas_call | solution.py:249
  134.6 0.0 collective-permute-done.5.refs_3_
  134.6 0.0 copy-done.1
  134.6 5.6 %attend_part.3.refs_4_ = f32[6,144,640]{2,1,0:T(8,128)} custom-call(s32[1]{0:T(128)} %bitcast.refs_0_, s32[1,64]{1,0:T(1,128)} %bitcast.24, bf16[3,128,1280]{2,1,0:T(8,128)(2,1)S(1)} %bitcast.16, bf16[4,128,128]{2,1,0:T(8,128)(2,1)S(1)} %collective-permute-done.5.refs_3_, bf16[2,4,128,128]{3,2,1,0:T(8,128)(2,1)S(1)} %collective-permute-done.2.refs_4_, ...), custom_call_target="tpu_custom_call" | custom-call | tf_op jit(solution)/shard_map/attend_part/pallas_call | solution.py:249
  140.3 0.0 collective-permute-done.3.refs_3_
  140.3 5.1 %attend_last.1 = bf16[3,128,1280]{2,1,0:T(8,128)(2,1)} custom-call(s32[1]{0:T(128)} %bitcast.refs_0_, s32[1,64]{1,0:T(1,128)} %bitcast.25, bf16[3,128,1280]{2,1,0:T(8,128)(2,1)S(1)} %bitcast.17, bf16[2,4,128,128]{3,2,1,0:T(8,128)(2,1)S(1)} %collective-permute-done.3.refs_3_, f32[6,144,640]{2,1,0:T(8,128)} %attend_part.3.refs_4_), custom_call_target="tpu_custom_call" | custom-call | tf_op jit(solution)/shard_map/attend_last/pallas_call | solution.py:249
  145.4 0.0 all-to-all-done
  145.4 2.0 %place_pages.1 = bf16[512,128]{1,0:T(8,128)(2,1)} custom-call(bf16[1280,128]{1,0:T(8,128)(2,1)S(1)} %bitcast.18), custom_call_target="tpu_custom_call" | custom-call | tf_op jit(solution)/shard_map/place_pages/pallas_call | solution.py:109
  (1 shorter events, 0.0 us)
Async XLA Ops:
  3.0 131.6 %copy-start.1 = (bf16[128,3,1280]{2,0,1:T(8,128)(2,1)S(1)}, bf16[128,3,1280]{2,0,1:T(8,128)(2,1)}, u32[]{:S(2)}) copy-start(bf16[128,3,1280]{2,0,1:T(8,128)(2,1)} %param.6) | copy-start | bytes 2949124
  3.0 142.4 %all-to-all-start = ((bf16[128,5,2,128]{3,2,1,0:T(2,128)(2,1)}), bf16[128,5,2,128]{3,2,1,0:T(2,128)(2,1)S(1)}, u32[]{:S(2)}, u32[]{:S(2)}) async-start(bf16[128,5,2,128]{3,2,1,0:T(2,128)(2,1)} %bitcast.8), calls=%async_computation | async-start | bytes 655360 | tf_op jit(solution)/shard_map/all_to_all | solution.py:272
  55.3 40.9 %collective-permute-start = (bf16[4,128,128]{2,1,0:T(8,128)(2,1)S(1)}, bf16[4,128,128]{2,1,0:T(8,128)(2,1)S(1)}, u32[]{:S(2)}, u32[]{:S(2)}) collective-permute-start(bf16[4,128,128]{2,1,0:T(8,128)(2,1)S(1)} %get-tuple-element.4.refs_3_), channel_id=1, source_target_pairs={{0,6},{2,8},{4,10},{6,12},{8,14},{10,16},{12,18},{14,20},{16,22},{... | collective-permute-start | bytes 393224 | tf_op jit(solution)/shard_map/ppermute | solution.py:32
  60.6 49.6 %collective-permute-start.1 = (bf16[4,128,128]{2,1,0:T(8,128)(2,1)S(1)}, bf16[4,128,128]{2,1,0:T(8,128)(2,1)S(1)}, u32[]{:S(2)}, u32[]{:S(2)}) collective-permute-start(bf16[4,128,128]{2,1,0:T(8,128)(2,1)S(1)} %get-tuple-element.4.refs_3_), channel_id=1, source_target_pairs={{0,12},{2,14},{4,16},{6,18},{8,20},{10,22},{12,24},{14,26},{16,28}... | collective-permute-start | bytes 393224 | tf_op jit(solution)/shard_map/ppermute | solution.py:32
  110.2 10.9 %collective-permute-start.2 = (bf16[2,4,128,128]{3,2,1,0:T(8,128)(2,1)S(1)}, bf16[2,4,128,128]{3,2,1,0:T(8,128)(2,1)S(1)}, u32[]{:S(2)}, u32[]{:S(2)}) collective-permute-start(bf16[2,4,128,128]{3,2,1,0:T(8,128)(2,1)S(1)} %pad_maximum_fusion), channel_id=1, source_target_pairs={{0,2},{2,4},{4,6},{6,8},{8,10},{10,12},{12,14},{14,16},{16,18},{18... | collective-permute-start | bytes 786440 | tf_op jit(solution)/shard_map/ppermute | solution.py:32
  114.6 10.7 %collective-permute-start.4 = (bf16[4,128,128]{2,1,0:T(8,128)(2,1)S(1)}, bf16[4,128,128]{2,1,0:T(8,128)(2,1)S(1)}, u32[]{:S(2)}, u32[]{:S(2)}) collective-permute-start(bf16[4,128,128]{2,1,0:T(8,128)(2,1)S(1)} %get-tuple-element.4.refs_3_), channel_id=1, source_target_pairs={{0,2},{2,4},{4,6},{6,8},{8,10},{10,12},{12,14},{14,16},{16,18},{18... | collective-permute-start | bytes 393224 | tf_op jit(solution)/shard_map/ppermute | solution.py:32
  121.1 19.1 %collective-permute-start.3 = (bf16[2,4,128,128]{3,2,1,0:T(8,128)(2,1)S(1)}, bf16[2,4,128,128]{3,2,1,0:T(8,128)(2,1)S(1)}, u32[]{:S(2)}, u32[]{:S(2)}) collective-permute-start(bf16[2,4,128,128]{3,2,1,0:T(8,128)(2,1)S(1)} %collective-permute-done.2.refs_4_), channel_id=1, source_target_pairs={{0,2},{2,4},{4,6},{6,8},{8,10},{10,12},{12,14},{14,16},{16,18},{18... | collective-permute-start | bytes 786440 | tf_op jit(solution)/shard_map/ppermute | solution.py:32
  125.3 9.3 %collective-permute-start.5 = (bf16[4,128,128]{2,1,0:T(8,128)(2,1)S(1)}, bf16[4,128,128]{2,1,0:T(8,128)(2,1)S(1)}, u32[]{:S(2)}, u32[]{:S(2)}) collective-permute-start(bf16[4,128,128]{2,1,0:T(8,128)(2,1)S(1)} %collective-permute-done.4.refs_4_), channel_id=1, source_target_pairs={{0,2},{2,4},{4,6},{6,8},{8,10},{10,12},{12,14},{14,16},{16,18},{18... | collective-permute-start | bytes 393224 | tf_op jit(solution)/shard_map/ppermute | solution.py:32
  127.6 1.2 copy-start
